TPU v7x, 256 devices: a whole 4x4x8 slice. The times are simulated.
256 devices in a mesh: blk: 128 (over y, z, x_hi, core), mp: 2 (over x_lo).
Axes of the slice: x: 4 (x_hi: 2, x_lo: 2; x = x_hi * 2 + x_lo), y: 4, z: 8, core: 2. Of those that a mesh axis runs over, the one named last changes fastest.
Arguments:
- params: bfloat16 [128, 1024, 4096], P('blk', None, 'mp'), may hold values from -0.09375 to 0.09375
- hidden: bfloat16 [128, 384, 4096], P('blk', None, 'mp'), may hold values from -6 to 6
- targets: bfloat16 [128, 384, 1024], P('blk', None, 'mp'), may hold values from -6 to 6
Outputs:
- params_out: bfloat16 [128, 1024, 4096], P('blk', None, 'mp')
- errors: float32 [2], replicated
All inputs are finite; a program needn't handle non-finite values.
Results may differ from a plain program's by a relative error of at most 0.0085.
Values may be sent and summed in bfloat16 or wider, within the bound.
A program may use at most 128 MiB of HBM per device.

v0:
```python
import functools
import jax
import jax.numpy as jnp
from jax import lax
from jax.sharding import Mesh
from jax.sharding import PartitionSpec as P

ITERS = 2
BLK = ("blk_0", "blk_1", "blk_2", "blk_3")
BLK_MP = ("blk_0", "blk_1", "blk_2", "blk_3", "mp")
mix_third = 1.0 / 3.0
step_size = 0.1


def from_behind(block, axis, distance):
    devices = range(lax.axis_size(axis))
    route = [((i - distance) % len(devices), i) for i in devices]
    return lax.ppermute(block, axis, route)


def from_everyone(x, axis):
    copies = jnp.broadcast_to(x, (lax.axis_size(axis), *x.shape))
    return lax.all_to_all(copies, axis, split_axis=0, concat_axis=0, tiled=True)


def taken_together(x, axis):
    return from_everyone(x, axis).sum(axis=0)


def over_axes(x, axes):
    return functools.reduce(lax.psum, axes, x)


def send_tracker(track):
    track_left = from_behind(track, BLK, 1)
    track_right = from_behind(track, BLK, -1)
    return (track_left, track_right)


def on_device(params, hidden, targets):
    state = params[0]
    feats = hidden[0]
    targ_local = targets[0]
    tokens = feats.shape[0]
    hidden_total = state.shape[1] * lax.axis_size("mp")
    replicas = lax.axis_size(BLK)
    full_targ = lax.all_gather(targ_local, "mp", axis=1, tiled=True)

    def gradient(weight):
        partial_value = lax.dot_general(
            feats, weight, (((1,), (1,)), ((), ())), preferred_element_type=jnp.float32
        )
        output = taken_together(partial_value, "mp")
        resid = (output - full_targ.astype(jnp.float32)).astype(jnp.bfloat16)
        grad = lax.dot_general(
            resid, feats, (((0,), (0,)), ((), ())), preferred_element_type=jnp.float32
        )
        return grad / tokens

    older = gradient(state)
    fresh = older
    track = older.astype(jnp.bfloat16)
    track_left, track_right = send_tracker(track)
    err_list = []
    for step in range(ITERS):
        state_left = from_behind(state, BLK, 1)
        state_right = from_behind(state, BLK, -1)
        if step > 0:
            track_mix = (
                track_left.astype(jnp.float32)
                + track.astype(jnp.float32)
                + track_right.astype(jnp.float32)
            ) * mix_third
            track = (track_mix + fresh - older).astype(jnp.bfloat16)
            older = fresh
        own_state = state.astype(jnp.float32)
        diff = own_state - state_right.astype(jnp.float32)
        local_err = jnp.sum(diff * diff) / (hidden_total * replicas)
        err_list.append(local_err)
        blended = (
            state_left.astype(jnp.float32) + own_state + state_right.astype(jnp.float32)
        ) * mix_third
        new_state = (blended - step_size * track.astype(jnp.float32)).astype(jnp.bfloat16)
        if step < ITERS - 1:
            fresh = gradient(new_state)
        state = new_state
    errors = jnp.stack(err_list)
    errors = over_axes(errors, BLK_MP)
    return (state[None], errors)


def solution(mesh):
    torus = Mesh(
        mesh.devices.reshape(4, 8, 2, 2, mesh.shape["mp"]),
        ("blk_0", "blk_1", "blk_2", "blk_3", "mp"),
    )
    placed = (P(BLK, None, "mp"), P(BLK, None, "mp"), P(BLK, None, "mp"))
    return jax.shard_map(
        on_device, mesh=torus, in_specs=placed, out_specs=(P(BLK, None, "mp"), P()), check_vma=False
    )
```

profile of v0, /device:TPU:194, one launch (start us, length us, event | category | flops | bytes accessed | tf_op | source)
XLA Modules:
  0.0 420.3 jit_solution(9891182136154639013)
XLA Ops:
  0.6 0.0 copy-start
  0.6 2.1 collective-permute-start.1
  2.7 0.0 collective-permute-start
  2.7 0.0 copy-done
  2.7 4.0 fusion.23
  6.8 2.1 broadcast_in_dim.9
  8.8 0.0 copy-start.2
  8.8 6.8 %all-to-all-start = ((f32[2,384,1024]{2,1,0:T(8,128)}), f32[2,384,1024]{2,1,0:T(8,128)}, u32[]{:S(2)}, u32[]{:S(2)}) async-start(f32[2,384,1024]{2,1,0:T(8,128)} %broadcast_in_dim.9), calls=%async_computation | async-start | bytes 6291456 | tf_op jit(solution)/shard_map/all_to_all | solution.py:23
  15.6 0.0 copy-done.2
  15.6 78.1 %all-gather = bf16[1,384,1024]{2,1,0:T(8,128)(2,1)} all-gather(bf16[1,384,512]{2,1,0:T(8,128)(2,1)S(1)} %copy-done.2), channel_id=2, replica_groups=mesh['blk_0'=4,'blk_1'=8,'blk_2'=2,'blk_3'=2,'mp'=2] {'mp'}, dimensions={2}, use_global_device_ids=true | all-gather | bytes 1179648 | tf_op jit(solution)/shard_map/all_gather | solution.py:47
  93.6 0.0 all-to-all-done
  93.6 2.3 reduce_sum.36
  96.0 0.0 collective-permute-done.1
  96.0 0.0 collective-permute-done
  96.0 13.7 %fusion.4 = (f32[]{:T(128)}, bf16[1024,2048]{1,0:T(8,128)(2,1)}, bf16[1024,2048]{1,0:T(8,128)(2,1)}, f32[1024,2048]{1,0:T(8,128)}) fusion(bf16[1024,2048]{1,0:T(8,128)(2,1)} %collective-permute-done.1, bf16[1,1024,2048]{2,1,0:T(8,128)(2,1)} %param.3, bf16[1024,2048]{1,0:T(8,128)(2,1)} %collective-permute-done, bf16[1,384,2048]{2,1,0:T(8,128)(2,1)S(1)} %copy-done, ...), kind=kOutput, calls=%fused_computation.12 | convolution fusion | flops 1643249664 | bytes 33292292 | tf_op jit(solution)/shard_map/dot_general | solution.py:55
  109.7 3.0 collective-permute-start.3
  112.7 86.1 %collective-permute-start.4 = (bf16[1024,2048]{1,0:T(8,128)(2,1)}, bf16[1024,2048]{1,0:T(8,128)(2,1)}, u32[]{:S(2)}, u32[]{:S(2)}) collective-permute-start(bf16[1024,2048]{1,0:T(8,128)(2,1)} %get-tuple-element.4), channel_id=1, source_target_pairs={{254,0},{0,2},{2,4},{4,6},{6,8},{8,10},{10,12},{12,14},{14,16},{16... | collective-permute-start | bytes 12582920 | tf_op jit(solution)/shard_map/ppermute | solution.py:18
  198.8 0.0 collective-permute-start.5
  198.8 3.2 collective-permute-start.2
  202.1 4.0 fusion.25
  206.1 2.1 broadcast_in_dim.10
  208.2 6.6 %all-to-all-start.1 = ((f32[2,384,1024]{2,1,0:T(8,128)}), f32[2,384,1024]{2,1,0:T(8,128)}, u32[]{:S(2)}, u32[]{:S(2)}) async-start(f32[2,384,1024]{2,1,0:T(8,128)} %broadcast_in_dim.10), calls=%async_computation.1 | async-start | bytes 6291456 | tf_op jit(solution)/shard_map/all_to_all | solution.py:23
  215.4 0.0 collective-permute-done.3
  215.4 6.3 %fusion.14 = f32[]{:T(128)} fusion(bf16[1024,2048]{1,0:T(8,128)(2,1)} %collective-permute-done.3, bf16[1024,2048]{1,0:T(8,128)(2,1)} %get-tuple-element.3), kind=kLoop, calls=%fused_computation.22 | loop fusion | flops 10485759 | bytes 8388612 | tf_op jit(solution)/shard_map/reduce_sum | solution.py:78
  221.7 0.0 copy-start.1
  222.4 0.1 pad_maximum_fusion
  222.5 10.7 %psum.35 = f32[2]{0:T(128)S(1)} all-reduce(f32[2]{0:T(128)S(1)} %pad_maximum_fusion), channel_id=1, replica_groups=mesh['blk_0'=4,'blk_1'=8,'blk_2'=2,'blk_3'=2,'mp'=2] {'blk_0'}, use_global_device_ids=true, to_apply=%region_4.0 | all-reduce | flops 2 | bytes 16 | tf_op jit(solution)/shard_map/psum | solution.py:31
  233.2 22.5 %psum.36 = f32[2]{0:T(128)S(1)} all-reduce(f32[2]{0:T(128)S(1)} %psum.35), channel_id=1, replica_groups=mesh['blk_0'=4,'blk_1'=8,'blk_2'=2,'blk_3'=2,'mp'=2] {'blk_1'}, use_global_device_ids=true, to_apply=%region_5.0 | all-reduce | flops 2 | bytes 16 | tf_op jit(solution)/shard_map/psum | solution.py:31
  255.7 138.1 %psum.37 = f32[2]{0:T(128)S(1)} all-reduce(f32[2]{0:T(128)S(1)} %psum.36), channel_id=1, replica_groups=mesh['blk_0'=4,'blk_1'=8,'blk_2'=2,'blk_3'=2,'mp'=2] {'blk_2'}, use_global_device_ids=true, to_apply=%region_6.0 | all-reduce | flops 2 | bytes 16 | tf_op jit(solution)/shard_map/psum | solution.py:31
  393.7 2.4 psum.38
  396.2 0.0 all-to-all-done.1
  396.2 3.5 reduce_sum.37
  399.6 5.4 %psum.39 = f32[2]{0:T(128)} all-reduce(f32[2]{0:T(128)S(1)} %psum.38), channel_id=1, replica_groups=mesh['blk_0'=4,'blk_1'=8,'blk_2'=2,'blk_3'=2,'mp'=2] {'mp'}, use_global_device_ids=true, to_apply=%region_8.0 | all-reduce | flops 2 | bytes 16 | tf_op jit(solution)/shard_map/psum | solution.py:31
  405.1 0.0 collective-permute-done.4
  405.1 0.0 collective-permute-done.5
  405.1 0.0 collective-permute-done.2
  405.1 0.0 copy-done.1
  405.1 15.3 %fusion.15 = bf16[1,1024,2048]{2,1,0:T(8,128)(2,1)} fusion(bf16[1024,2048]{1,0:T(8,128)(2,1)} %collective-permute-done.3, bf16[1024,2048]{1,0:T(8,128)(2,1)} %get-tuple-element.3, bf16[1024,2048]{1,0:T(8,128)(2,1)} %collective-permute-done.2, f32[1024,2048]{1,0:T(8,128)} %get-tuple-element.5, bf16[1024,2048]{1,0:T(8,128)(2,1)} %collective-permute-done.5, ...), kind=kOutput, calls=%fused_computation.24 | convolution fusion | flops 1657929728 | bytes 37486592 | tf_op jit(solution)/shard_map/dot_general | solution.py:55
Async XLA Ops:
  0.6 2.1 copy-start
  0.6 95.3 %collective-permute-start.1 = (bf16[1024,2048]{1,0:T(8,128)(2,1)}, bf16[1024,2048]{1,0:T(8,128)(2,1)}, u32[]{:S(2)}, u32[]{:S(2)}) collective-permute-start(bf16[1024,2048]{1,0:T(8,128)(2,1)} %bitcast.37), channel_id=1, source_target_pairs={{2,0},{4,2},{6,4},{8,6},{10,8},{12,10},{14,12},{16,14},{18,16},{20... | collective-permute-start | bytes 12582920 | tf_op jit(solution)/shard_map/ppermute | solution.py:18
  2.7 93.2 %collective-permute-start = (bf16[1024,2048]{1,0:T(8,128)(2,1)}, bf16[1024,2048]{1,0:T(8,128)(2,1)}, u32[]{:S(2)}, u32[]{:S(2)}) collective-permute-start(bf16[1024,2048]{1,0:T(8,128)(2,1)} %bitcast.38), channel_id=1, source_target_pairs={{254,0},{0,2},{2,4},{4,6},{6,8},{8,10},{10,12},{12,14},{14,16},{16... | collective-permute-start | bytes 12582920 | tf_op jit(solution)/shard_map/ppermute | solution.py:18
  8.8 6.8 %copy-start.2 = (bf16[1,384,512]{2,1,0:T(8,128)(2,1)S(1)}, bf16[1,384,512]{2,1,0:T(8,128)(2,1)}, u32[]{:S(2)}) copy-start(bf16[1,384,512]{2,1,0:T(8,128)(2,1)} %param.5) | copy-start | bytes 1179652
  8.8 84.8 %all-to-all-start = ((f32[2,384,1024]{2,1,0:T(8,128)}), f32[2,384,1024]{2,1,0:T(8,128)}, u32[]{:S(2)}, u32[]{:S(2)}) async-start(f32[2,384,1024]{2,1,0:T(8,128)} %broadcast_in_dim.9), calls=%async_computation | async-start | bytes 6291456 | tf_op jit(solution)/shard_map/all_to_all | solution.py:23
  109.7 105.7 %collective-permute-start.3 = (bf16[1024,2048]{1,0:T(8,128)(2,1)}, bf16[1024,2048]{1,0:T(8,128)(2,1)}, u32[]{:S(2)}, u32[]{:S(2)}) collective-permute-start(bf16[1024,2048]{1,0:T(8,128)(2,1)} %get-tuple-element.3), channel_id=1, source_target_pairs={{2,0},{4,2},{6,4},{8,6},{10,8},{12,10},{14,12},{16,14},{18,16},{20... | collective-permute-start | bytes 12582920 | tf_op jit(solution)/shard_map/ppermute | solution.py:18
  112.7 292.4 %collective-permute-start.4 = (bf16[1024,2048]{1,0:T(8,128)(2,1)}, bf16[1024,2048]{1,0:T(8,128)(2,1)}, u32[]{:S(2)}, u32[]{:S(2)}) collective-permute-start(bf16[1024,2048]{1,0:T(8,128)(2,1)} %get-tuple-element.4), channel_id=1, source_target_pairs={{254,0},{0,2},{2,4},{4,6},{6,8},{8,10},{10,12},{12,14},{14,16},{16... | collective-permute-start | bytes 12582920 | tf_op jit(solution)/shard_map/ppermute | solution.py:18
  198.8 206.2 %collective-permute-start.5 = (bf16[1024,2048]{1,0:T(8,128)(2,1)}, bf16[1024,2048]{1,0:T(8,128)(2,1)}, u32[]{:S(2)}, u32[]{:S(2)}) collective-permute-start(bf16[1024,2048]{1,0:T(8,128)(2,1)} %get-tuple-element.4), channel_id=1, source_target_pairs={{2,0},{4,2},{6,4},{8,6},{10,8},{12,10},{14,12},{16,14},{18,16},{20... | collective-permute-start | bytes 12582920 | tf_op jit(solution)/shard_map/ppermute | solution.py:18
  198.8 206.2 %collective-permute-start.2 = (bf16[1024,2048]{1,0:T(8,128)(2,1)}, bf16[1024,2048]{1,0:T(8,128)(2,1)}, u32[]{:S(2)}, u32[]{:S(2)}) collective-permute-start(bf16[1024,2048]{1,0:T(8,128)(2,1)} %get-tuple-element.3), channel_id=1, source_target_pairs={{254,0},{0,2},{2,4},{4,6},{6,8},{8,10},{10,12},{12,14},{14,16},{16... | collective-permute-start | bytes 12582920 | tf_op jit(solution)/shard_map/ppermute | solution.py:18
  208.2 188.0 %all-to-all-start.1 = ((f32[2,384,1024]{2,1,0:T(8,128)}), f32[2,384,1024]{2,1,0:T(8,128)}, u32[]{:S(2)}, u32[]{:S(2)}) async-start(f32[2,384,1024]{2,1,0:T(8,128)} %broadcast_in_dim.10), calls=%async_computation.1 | async-start | bytes 6291456 | tf_op jit(solution)/shard_map/all_to_all | solution.py:23
  221.7 183.4 %copy-start.1 = (bf16[1,384,1024]{2,1,0:T(8,128)(2,1)S(1)}, bf16[1,384,1024]{2,1,0:T(8,128)(2,1)}, u32[]{:S(2)}) copy-start(bf16[1,384,1024]{2,1,0:T(8,128)(2,1)} %all-gather) | copy-start | bytes 2359300
where the time goes:
time: 421 us; the launch traced here: 420 us
  blocking collectives  257 us (61%)
  starting transfers between devices  108 us (26%)
  matrix products  37.1 us (9%)
  other arithmetic  12.1 us (3%)
    psum x5, blocking collectives, over_axes(): return functools.reduce(lax.psum, axes, x)  179 us
    ppermute x6, starting transfers between devices, from_behind(): return lax.ppermute(block, axis, route)  94.4 us
    all_gather x1, blocking collectives, on_device(): full_targ = lax.all_gather(targ_local, 'mp', axis=1, tiled=True)  78.1 us
    dot_general x2, matrix products, gradient(): lax.dot_general(resid, feats, (((0,), (0,)), ((), ())), preferred_element...  29 us
    all_to_all x2, starting transfers between devices, from_everyone(): return lax.all_to_all(copies, axis, split_axis=0, concat_axis=0, tiled=True)  13.3 us
  transfers between devices with their start and end apart: 8, of which 0 were waited for; matrix products, arithmetic and copies ran while one was open for 6% of the time, Pallas kernels for 0%

commit v1 on v0

--- a/solution.py
+++ b/solution.py
@@ -44,7 +44,12 @@
     tokens = feats.shape[0]
     hidden_total = state.shape[1] * lax.axis_size("mp")
     replicas = lax.axis_size(BLK)
-    full_targ = lax.all_gather(targ_local, "mp", axis=1, tiled=True)
+    full_targ = jnp.concatenate(
+        lax.all_to_all(
+            jnp.stack([targ_local for _ in range(lax.axis_size("mp"))], axis=0), "mp", 0, 0
+        ),
+        axis=1,
+    )
 
     def gradient(weight):
         partial_value = lax.dot_general(

time: 421 us -> 416 us (0.988); the launches traced: 420 us -> 411 us
  blocking collectives: 257 us -> 130 us
  waiting for transfers between devices: 0.02 us -> 97.4 us
  local copies, waits for them, and re-layouts: 4.16 us -> 14.9 us
  other arithmetic: 12.1 us -> 17.3 us
  starting transfers between devices: 108 us -> 113 us
    all_to_all x2, waiting for transfers between devices: 0.01 us -> 93.7 us  [from_everyone(): return lax.all_to_all(copies, axis, split_axis=0, concat_axis=0, tiled=True)]
    all_gather x1 -> x0, blocking collectives: 78.1 us -> none  [on_device(): full_targ = lax.all_gather(targ_local, 'mp', axis=1, tiled=True)]
    psum x5, blocking collectives: 179 us -> 130 us  [over_axes(): return functools.reduce(lax.psum, axes, x)]
    reduce_sum x0 -> x2, local copies, waits for them, and re-layouts: none -> 6.1 us  [taken_together(): return from_everyone(x, axis).sum(axis=0)]
  transfers between devices with their start and end apart: 8 -> 9, of which waited for: 0 -> 3; matrix products, arithmetic and copies ran while one was open for 6% -> 10% of each run, Pallas kernels for 0% -> 0%
where the time goes in v1:
time: 416 us; the launch traced here: 411 us
  blocking collectives  130 us (31%)
  starting transfers between devices  113 us (27%)
  waiting for transfers between devices  97.4 us (23%)
  matrix products  36.2 us (9%)
  other arithmetic  17.3 us (4%)
  local copies, waits for them, and re-layouts  14.9 us (4%)
    psum x5, blocking collectives, over_axes(): return functools.reduce(lax.psum, axes, x)  130 us
    ppermute x6, starting transfers between devices, from_behind(): return lax.ppermute(block, axis, route)  95.4 us
    all_to_all x2, waiting for transfers between devices, from_everyone(): return lax.all_to_all(copies, axis, split_axis=0, concat_axis=0, tiled=True)  93.7 us
    dot_general x2, matrix products, gradient(): lax.dot_general(resid, feats, (((0,), (0,)), ((), ())), preferred_element...  26.5 us
    all_to_all x2, starting transfers between devices, from_everyone(): return lax.all_to_all(copies, axis, split_axis=0, concat_axis=0, tiled=True)  13 us
    dot_general x2, matrix products, gradient(): lax.dot_general(feats, weight, (((1,), (1,)), ((), ())), preferred_elemen...  9.7 us
  transfers between devices with their start and end apart: 9, of which 3 were waited for; matrix products, arithmetic and copies ran while one was open for 10% of the time, Pallas kernels for 0%

profile of v1, /device:TPU:194, one launch (start us, length us, event | category | flops | bytes accessed | tf_op | source)
XLA Modules:
  0.0 410.6 jit_solution(8935733535594329587)
XLA Ops:
  0.6 0.0 copy-start
  0.6 2.1 collective-permute-start.1
  2.7 0.0 collective-permute-start
  2.7 0.0 copy-done
  2.7 4.0 fusion.23
  6.8 2.1 broadcast_in_dim.9
  8.8 0.0 copy-start.1
  8.8 6.8 %all-to-all-start = ((f32[2,384,1024]{2,1,0:T(8,128)}), f32[2,384,1024]{2,1,0:T(8,128)}, u32[]{:S(2)}, u32[]{:S(2)}) async-start(f32[2,384,1024]{2,1,0:T(8,128)} %broadcast_in_dim.9), calls=%async_computation | async-start | bytes 6291456 | tf_op jit(solution)/shard_map/all_to_all | solution.py:23
  15.6 0.0 copy-done.1
  15.6 0.2 copy.10
  15.8 1.0 pad_maximum_fusion
  16.8 68.4 %all-to-all-done = f32[2,384,1024]{2,1,0:T(8,128)} async-done(((f32[2,384,1024]{2,1,0:T(8,128)}), f32[2,384,1024]{2,1,0:T(8,128)}, u32[]{:S(2)}, u32[]{:S(2)}) %all-to-all-start) | async-done | bytes 3145760 | tf_op jit(solution)/shard_map/all_to_all | solution.py:23
  85.2 4.1 %all-to-all-start.1 = ((bf16[2,384,512]{1,2,0:T(8,128)(2,1)}), bf16[2,384,512]{1,2,0:T(8,128)(2,1)S(1)}, u32[]{:S(2)}, u32[]{:S(2)}) async-start(bf16[2,384,512]{1,2,0:T(8,128)(2,1)} %pad_maximum_fusion), calls=%async_computation.1 | async-start | bytes 1572864 | tf_op jit(solution)/shard_map/all_to_all | solution.py:48
  89.3 3.5 reduce_sum.40
  92.8 3.0 copy.9
  95.8 3.7 all-to-all-done.1
  99.5 1.6 fusion.16
  101.1 0.0 collective-permute-done.1
  101.1 0.0 collective-permute-done
  101.1 12.1 %fusion.4 = (f32[]{:T(128)}, bf16[1024,2048]{1,0:T(8,128)(2,1)}, bf16[1024,2048]{1,0:T(8,128)(2,1)}, f32[1024,2048]{1,0:T(8,128)}) fusion(bf16[1024,2048]{1,0:T(8,128)(2,1)} %collective-permute-done.1, bf16[1,1024,2048]{2,1,0:T(8,128)(2,1)} %param.3, bf16[1024,2048]{1,0:T(8,128)(2,1)} %collective-permute-done, bf16[384,1024]{0,1:T(8,128)(2,1)S(1)} %bitcast.42, ...), kind=kOutput, calls=%fused_computation.12 | convolution fusion | flops 1642070016 | bytes 31719428 | tf_op jit(solution)/shard_map/dot_general | solution.py:60
  113.2 3.1 collective-permute-start.3
  116.3 87.0 %collective-permute-start.4 = (bf16[1024,2048]{1,0:T(8,128)(2,1)}, bf16[1024,2048]{1,0:T(8,128)(2,1)}, u32[]{:S(2)}, u32[]{:S(2)}) collective-permute-start(bf16[1024,2048]{1,0:T(8,128)(2,1)} %get-tuple-element.4), channel_id=1, source_target_pairs={{254,0},{0,2},{2,4},{4,6},{6,8},{8,10},{10,12},{12,14},{14,16},{16... | collective-permute-start | bytes 12582920 | tf_op jit(solution)/shard_map/ppermute | solution.py:18
  203.3 0.0 collective-permute-start.5
  203.3 3.2 collective-permute-start.2
  206.5 5.7 %fusion.25 = f32[384,1024]{0,1:T(8,128)} fusion(bf16[1024,2048]{1,0:T(8,128)(2,1)} %get-tuple-element.3, bf16[1,384,2048]{2,1,0:T(8,128)(2,1)S(1)} %copy-done), kind=kOutput, calls=%fused_computation.36 | convolution fusion | flops 1610612736 | bytes 7340032 | tf_op jit(solution)/shard_map/dot_general | solution.py:55
  212.2 3.1 copy.12
  215.3 3.5 broadcast_in_dim.10
  218.8 6.3 %all-to-all-start.2 = ((f32[2,384,1024]{2,1,0:T(8,128)}), f32[2,384,1024]{2,1,0:T(8,128)}, u32[]{:S(2)}, u32[]{:S(2)}) async-start(f32[2,384,1024]{2,1,0:T(8,128)} %broadcast_in_dim.10), calls=%async_computation.2 | async-start | bytes 6291456 | tf_op jit(solution)/shard_map/all_to_all | solution.py:23
  225.7 0.0 collective-permute-done.3
  225.7 6.3 %fusion.14 = f32[]{:T(128)} fusion(bf16[1024,2048]{1,0:T(8,128)(2,1)} %collective-permute-done.3, bf16[1024,2048]{1,0:T(8,128)(2,1)} %get-tuple-element.3), kind=kLoop, calls=%fused_computation.22 | loop fusion | flops 10485759 | bytes 8388612 | tf_op jit(solution)/shard_map/reduce_sum | solution.py:83
  232.6 0.1 pad_maximum_fusion.1
  232.7 10.7 %psum.35 = f32[2]{0:T(128)S(1)} all-reduce(f32[2]{0:T(128)S(1)} %pad_maximum_fusion.1), channel_id=1, replica_groups=mesh['blk_0'=4,'blk_1'=8,'blk_2'=2,'blk_3'=2,'mp'=2] {'blk_0'}, use_global_device_ids=true, to_apply=%region_4.0 | all-reduce | flops 2 | bytes 16 | tf_op jit(solution)/shard_map/psum | solution.py:31
  243.4 16.7 %psum.36 = f32[2]{0:T(128)S(1)} all-reduce(f32[2]{0:T(128)S(1)} %psum.35), channel_id=1, replica_groups=mesh['blk_0'=4,'blk_1'=8,'blk_2'=2,'blk_3'=2,'mp'=2] {'blk_1'}, use_global_device_ids=true, to_apply=%region_5.0 | all-reduce | flops 2 | bytes 16 | tf_op jit(solution)/shard_map/psum | solution.py:31
  260.1 25.3 %all-to-all-done.2 = f32[2,384,1024]{2,1,0:T(8,128)} async-done(((f32[2,384,1024]{2,1,0:T(8,128)}), f32[2,384,1024]{2,1,0:T(8,128)}, u32[]{:S(2)}, u32[]{:S(2)}) %all-to-all-start.2) | async-done | bytes 3145760 | tf_op jit(solution)/shard_map/all_to_all | solution.py:23
  285.4 3.5 reduce_sum.42
  288.8 94.7 %psum.37 = f32[2]{0:T(128)S(1)} all-reduce(f32[2]{0:T(128)S(1)} %psum.36), channel_id=1, replica_groups=mesh['blk_0'=4,'blk_1'=8,'blk_2'=2,'blk_3'=2,'mp'=2] {'blk_2'}, use_global_device_ids=true, to_apply=%region_6.0 | all-reduce | flops 2 | bytes 16 | tf_op jit(solution)/shard_map/psum | solution.py:31
  383.6 3.1 copy.13
  386.6 2.4 psum.38
  389.1 1.6 fusion.17
  390.6 5.6 %psum.39 = f32[2]{0:T(128)} all-reduce(f32[2]{0:T(128)S(1)} %psum.38), channel_id=1, replica_groups=mesh['blk_0'=4,'blk_1'=8,'blk_2'=2,'blk_3'=2,'mp'=2] {'mp'}, use_global_device_ids=true, to_apply=%region_8.0 | all-reduce | flops 2 | bytes 16 | tf_op jit(solution)/shard_map/psum | solution.py:31
  396.3 0.0 collective-permute-done.4
  396.3 0.0 collective-permute-done.5
  396.3 0.0 collective-permute-done.2
  396.3 14.4 %fusion.15 = bf16[1,1024,2048]{2,1,0:T(8,128)(2,1)} fusion(bf16[1024,2048]{1,0:T(8,128)(2,1)} %collective-permute-done.3, bf16[1024,2048]{1,0:T(8,128)(2,1)} %get-tuple-element.3, bf16[1024,2048]{1,0:T(8,128)(2,1)} %collective-permute-done.2, f32[1024,2048]{1,0:T(8,128)} %get-tuple-element.5, bf16[384,1024]{0,1:T(8,128)(2,1)S(1)} %bitcast.43, ...), kind=kOutput, calls=%fused_computation.24 | convolution fusion | flops 1656750080 | bytes 35913728 | tf_op jit(solution)/shard_map/dot_general | solution.py:60
Async XLA Ops:
  0.6 2.1 copy-start
  0.6 100.4 %collective-permute-start.1 = (bf16[1024,2048]{1,0:T(8,128)(2,1)}, bf16[1024,2048]{1,0:T(8,128)(2,1)}, u32[]{:S(2)}, u32[]{:S(2)}) collective-permute-start(bf16[1024,2048]{1,0:T(8,128)(2,1)} %bitcast.40), channel_id=1, source_target_pairs={{2,0},{4,2},{6,4},{8,6},{10,8},{12,10},{14,12},{16,14},{18,16},{20... | collective-permute-start | bytes 12582920 | tf_op jit(solution)/shard_map/ppermute | solution.py:18
  2.7 98.4 %collective-permute-start = (bf16[1024,2048]{1,0:T(8,128)(2,1)}, bf16[1024,2048]{1,0:T(8,128)(2,1)}, u32[]{:S(2)}, u32[]{:S(2)}) collective-permute-start(bf16[1024,2048]{1,0:T(8,128)(2,1)} %bitcast.41), channel_id=1, source_target_pairs={{254,0},{0,2},{2,4},{4,6},{6,8},{8,10},{10,12},{12,14},{14,16},{16... | collective-permute-start | bytes 12582920 | tf_op jit(solution)/shard_map/ppermute | solution.py:18
  8.8 6.8 %copy-start.1 = (bf16[1,384,512]{2,1,0:T(8,128)(2,1)S(1)}, bf16[1,384,512]{2,1,0:T(8,128)(2,1)}, u32[]{:S(2)}) copy-start(bf16[1,384,512]{2,1,0:T(8,128)(2,1)} %param.5) | copy-start | bytes 1179652
  8.8 76.4 %all-to-all-start = ((f32[2,384,1024]{2,1,0:T(8,128)}), f32[2,384,1024]{2,1,0:T(8,128)}, u32[]{:S(2)}, u32[]{:S(2)}) async-start(f32[2,384,1024]{2,1,0:T(8,128)} %broadcast_in_dim.9), calls=%async_computation | async-start | bytes 6291456 | tf_op jit(solution)/shard_map/all_to_all | solution.py:23
  85.2 14.3 %all-to-all-start.1 = ((bf16[2,384,512]{1,2,0:T(8,128)(2,1)}), bf16[2,384,512]{1,2,0:T(8,128)(2,1)S(1)}, u32[]{:S(2)}, u32[]{:S(2)}) async-start(bf16[2,384,512]{1,2,0:T(8,128)(2,1)} %pad_maximum_fusion), calls=%async_computation.1 | async-start | bytes 1572864 | tf_op jit(solution)/shard_map/all_to_all | solution.py:48
  113.2 112.5 %collective-permute-start.3 = (bf16[1024,2048]{1,0:T(8,128)(2,1)}, bf16[1024,2048]{1,0:T(8,128)(2,1)}, u32[]{:S(2)}, u32[]{:S(2)}) collective-permute-start(bf16[1024,2048]{1,0:T(8,128)(2,1)} %get-tuple-element.3), channel_id=1, source_target_pairs={{2,0},{4,2},{6,4},{8,6},{10,8},{12,10},{14,12},{16,14},{18,16},{20... | collective-permute-start | bytes 12582920 | tf_op jit(solution)/shard_map/ppermute | solution.py:18
  116.3 279.9 %collective-permute-start.4 = (bf16[1024,2048]{1,0:T(8,128)(2,1)}, bf16[1024,2048]{1,0:T(8,128)(2,1)}, u32[]{:S(2)}, u32[]{:S(2)}) collective-permute-start(bf16[1024,2048]{1,0:T(8,128)(2,1)} %get-tuple-element.4), channel_id=1, source_target_pairs={{254,0},{0,2},{2,4},{4,6},{6,8},{8,10},{10,12},{12,14},{14,16},{16... | collective-permute-start | bytes 12582920 | tf_op jit(solution)/shard_map/ppermute | solution.py:18
  203.3 193.0 %collective-permute-start.5 = (bf16[1024,2048]{1,0:T(8,128)(2,1)}, bf16[1024,2048]{1,0:T(8,128)(2,1)}, u32[]{:S(2)}, u32[]{:S(2)}) collective-permute-start(bf16[1024,2048]{1,0:T(8,128)(2,1)} %get-tuple-element.4), channel_id=1, source_target_pairs={{2,0},{4,2},{6,4},{8,6},{10,8},{12,10},{14,12},{16,14},{18,16},{20... | collective-permute-start | bytes 12582920 | tf_op jit(solution)/shard_map/ppermute | solution.py:18
  203.3 193.0 %collective-permute-start.2 = (bf16[1024,2048]{1,0:T(8,128)(2,1)}, bf16[1024,2048]{1,0:T(8,128)(2,1)}, u32[]{:S(2)}, u32[]{:S(2)}) collective-permute-start(bf16[1024,2048]{1,0:T(8,128)(2,1)} %get-tuple-element.3), channel_id=1, source_target_pairs={{254,0},{0,2},{2,4},{4,6},{6,8},{8,10},{10,12},{12,14},{14,16},{16... | collective-permute-start | bytes 12582920 | tf_op jit(solution)/shard_map/ppermute | solution.py:18
  218.8 66.6 %all-to-all-start.2 = ((f32[2,384,1024]{2,1,0:T(8,128)}), f32[2,384,1024]{2,1,0:T(8,128)}, u32[]{:S(2)}, u32[]{:S(2)}) async-start(f32[2,384,1024]{2,1,0:T(8,128)} %broadcast_in_dim.10), calls=%async_computation.2 | async-start | bytes 6291456 | tf_op jit(solution)/shard_map/all_to_all | solution.py:23
